TPU v7x, 32 devices: a whole 2x2x4 slice. The times are simulated.
32 devices in a mesh: samp: 4 (over x, core), snp: 8 (over z, y).
Axes of the slice: x: 2, y: 2, z: 4, core: 2. Of those that a mesh axis runs over, the one named last changes fastest.
Arguments:
- genotype: bfloat16 [40960, 40960], P('samp', 'snp'), may hold values from 0 to 2, as said below
- centre: float32 [40960], P('snp'), may hold values from 0.1 to 1
- spread: float32 [40960], P('snp'), may hold values from 0.308 to 0.7072
- pheno_probes: float32 [32, 40960], P(None, ('samp', 'snp')), may hold values from -15.75 to 15.75
Outputs:
- solution: float32 [32, 40960], P(None, ('samp', 'snp'))
- marker_stats: float32 [32, 40960], P(None, 'snp')
Inputs may be any that keep to these rules, and one draw needn't show every extreme that they name: `genotype`: whole numbers.
All inputs are finite; a program needn't handle non-finite values.
Results may differ from a plain program's by a relative error of at most 0.0003.
Values sent between devices are 32-bit elements; how exact they have to be, the bound alone decides.
A program may use at most 448 MiB of HBM per device.

v0:
```python
import math
import jax
import jax.numpy as jnp
from jax import lax
from jax.sharding import PartitionSpec as P

ROUNDS = 3
RIDGE = 0.1
LANES = 128


def split(values):
    high = lax.reduce_precision(values, 8, 7)
    low = lax.reduce_precision(values - high, 8, 7)
    return (jnp.concatenate([high, low], axis=0).astype(jnp.bfloat16), high + low)


def product(pieces, genotype, dimension):
    rows = pieces.shape[0] // 2
    pieces = lax.dot_general(
        pieces, genotype, (((1,), (dimension,)), ((), ())), preferred_element_type=jnp.float32
    )
    return pieces[:rows] + pieces[rows:]


def row_sum(values):
    return jnp.sum(values, axis=1, keepdims=True)


def with_scalars(values, scalars):
    rows = values.shape[0]
    filler = jnp.zeros((rows, LANES - len(scalars)), jnp.float32)
    return jnp.concatenate([values, *scalars, filler], axis=1)


def local(samples, markers, genotype, centre, spread, pheno_probes):
    shard = pheno_probes.shape[1]
    columns = genotype.shape[1]
    block = genotype.shape[0]
    first = lax.axis_index("snp") * shard
    inverse = 1.0 / spread[None, :]
    middle = centre[None, :]
    residual = lax.all_gather(pheno_probes, "snp", axis=1, tiled=True)
    direction = load = norm = square = None
    solution = stats = None
    for counter in range(ROUNDS):
        pieces, rounded = split(residual)
        scalars = [row_sum(rounded), row_sum(residual * residual)]
        if counter:
            scalars.append(row_sum(residual * direction))
        raw = product(pieces, genotype, 0)
        total = lax.psum(with_scalars(raw, scalars), "samp")
        residual_load = (total[:, :columns] - total[:, columns : columns + 1] * middle) * inverse
        norm_next = total[:, columns + 1 : columns + 2]
        if counter:
            ratio = norm_next / norm
            cross = total[:, columns + 2 : columns + 3]
            load = residual_load + ratio * load
            direction = residual + ratio * direction
            square = norm_next + 2.0 * ratio * cross + ratio * ratio * square
        else:
            load, direction, square = (residual_load, residual, norm_next)
        norm = norm_next
        power = row_sum(load * load)
        if counter < ROUNDS - 1:
            pieces, rounded = split(load * inverse)
            image = product(pieces, genotype, 1) - row_sum(rounded * middle)
            summed = lax.psum(with_scalars(image, [power]), "snp")
            power = summed[:, block : block + 1]
        else:
            power = lax.psum(power, "snp")
        step = norm / (power / markers + RIDGE * square)
        own = lax.dynamic_slice_in_dim(direction, first, shard, 1)
        solution = step * own if solution is None else solution + step * own
        stats = step * load if stats is None else stats + step * load
        if counter < ROUNDS - 1:
            applied = summed[:, :block] / markers + RIDGE * direction
            residual = residual - step * applied
    return (solution, stats / math.sqrt(samples))


def solution(mesh):
    in_specs = (P("samp", "snp"), P("snp"), P("snp"), P(None, ("samp", "snp")))
    out_specs = (P(None, ("samp", "snp")), P(None, "snp"))

    def whole(genotype, centre, spread, pheno_probes):
        samples, markers = genotype.shape

        def body(*blocks):
            return local(samples, markers, *blocks)

        return jax.shard_map(
            body, mesh=mesh, in_specs=in_specs, out_specs=out_specs, check_vma=False
        )(genotype, centre, spread, pheno_probes)

    return whole
```

profile of v0, /device:TPU:0, one launch (start us, length us, event | category | flops | bytes accessed | tf_op | source)
XLA Modules:
  0.0 597.3 jit_solution(6193682254995479344)
XLA Ops:
  7.9 46.8 %all-gather.2.cloned.1.call-done = f32[32,10240]{1,0:T(8,128)} async-done(((f32[32,1280]{1,0:T(8,128)}), f32[32,10240]{1,0:T(8,128)}) %all-gather.2.cloned.1.call-update) | async-done | bytes 1310736 | tf_op jit(solution)/shard_map/all_gather | solution.py:43
  54.7 1.8 multiply_reduce_fusion.4
  56.5 35.8 %fusion.17 = f32[64,5120]{1,0:T(8,128)S(1)} fusion(bf16[10240,5120]{1,0:T(8,128)(2,1)} %param.4, bf16[32,10240]{1,0:T(8,128)(2,1)S(1)} %get-tuple-element.26, bf16[32,10240]{1,0:T(8,128)(2,1)S(1)} %get-tuple-element.27), kind=kOutput, calls=%fused_computation.30 | convolution fusion | flops 6713507840 | bytes 107479040 | tf_op jit(solution)/shard_map/dot_general | solution.py:20
  93.6 32.9 %all-reduce.6.cloned.1.call-done = f32[32,5248]{1,0:T(8,128)} async-done(((f32[32,5248]{1,0:T(8,128)}), f32[32,5248]{1,0:T(8,128)}) %all-reduce.6.cloned.1.call-update) | async-done | bytes 671760 | tf_op jit(solution)/shard_map/psum | solution.py:52
  127.3 1.5 multiply_reduce_fusion.7
  128.9 39.7 %fusion.42 = f32[64,10240]{1,0:T(8,128)S(1)} fusion(bf16[10240,5120]{1,0:T(8,128)(2,1)} %param.4, bf16[32,5120]{1,0:T(8,128)(2,1)S(1)} %get-tuple-element.29, bf16[32,5120]{1,0:T(8,128)(2,1)S(1)} %get-tuple-element.28), kind=kOutput, calls=%fused_computation.73 | convolution fusion | flops 6712197120 | bytes 108134400 | tf_op jit(solution)/shard_map/dot_general | solution.py:20
  168.6 1.2 fusion.16
  169.8 2.3 concatenate.38
  172.2 84.1 %all-reduce.8.cloned.1.call-done = f32[32,10368]{1,0:T(8,128)} async-done(((f32[32,10368]{1,0:T(8,128)}), f32[32,10368]{1,0:T(8,128)}) %all-reduce.8.cloned.1.call-update) | async-done | bytes 1327120 | tf_op jit(solution)/shard_map/psum | solution.py:68
  257.2 2.1 multiply_reduce_fusion.2
  259.3 1.0 reduce-precision_convert_fusion.1
  260.3 37.0 %fusion.21 = f32[64,5120]{1,0:T(8,128)} fusion(bf16[10240,5120]{1,0:T(8,128)(2,1)} %param.4, bf16[32,10240]{1,0:T(8,128)(2,1)} %get-tuple-element.25, bf16[32,10240]{1,0:T(8,128)(2,1)S(1)} %get-tuple-element.24), kind=kOutput, calls=%fused_computation.34 | convolution fusion | flops 6713507840 | bytes 107479040 | tf_op jit(solution)/shard_map/dot_general | solution.py:20
  297.3 1.4 slice_add_fusion.3
  300.1 33.0 %all-reduce.10.cloned.1.call-done = f32[32,5248]{1,0:T(8,128)} async-done(((f32[32,5248]{1,0:T(8,128)}), f32[32,5248]{1,0:T(8,128)}) %all-reduce.10.cloned.1.call-update) | async-done | bytes 671760 | tf_op jit(solution)/shard_map/psum | solution.py:52
  333.1 1.0 slice_reduce_fusion.1
  334.1 1.8 multiply_reduce_fusion.6
  337.0 40.9 %fusion.46 = f32[64,10240]{1,0:T(8,128)} fusion(bf16[10240,5120]{1,0:T(8,128)(2,1)} %param.4, bf16[32,5120]{1,0:T(8,128)(2,1)} %get-tuple-element.31, bf16[32,5120]{1,0:T(8,128)(2,1)} %get-tuple-element.30), kind=kOutput, calls=%fused_computation.77 | convolution fusion | flops 6712197120 | bytes 108134400 | tf_op jit(solution)/shard_map/dot_general | solution.py:20
  377.9 3.0 fusion.12
  380.9 2.3 concatenate.42
  383.2 84.1 %all-reduce.12.cloned.1.call-done = f32[32,10368]{1,0:T(8,128)} async-done(((f32[32,10368]{1,0:T(8,128)}), f32[32,10368]{1,0:T(8,128)}) %all-reduce.12.cloned.1.call-update) | async-done | bytes 1327120 | tf_op jit(solution)/shard_map/psum | solution.py:68
  467.3 1.0 fusion.64
  468.3 3.3 multiply_reduce_fusion
  471.6 1.4 reduce-precision_convert_fusion
  473.1 36.2 %fusion.25 = f32[64,5120]{1,0:T(8,128)S(1)} fusion(bf16[10240,5120]{1,0:T(8,128)(2,1)} %param.4, bf16[32,10240]{1,0:T(8,128)(2,1)} %get-tuple-element.23, bf16[32,10240]{1,0:T(8,128)(2,1)} %get-tuple-element.22), kind=kOutput, calls=%fused_computation.38 | convolution fusion | flops 6713507840 | bytes 107479040 | tf_op jit(solution)/shard_map/dot_general | solution.py:20
  510.5 2.1 concatenate.44
  512.5 33.2 %all-reduce.14.cloned.1.call-done = f32[32,5248]{1,0:T(8,128)} async-done(((f32[32,5248]{1,0:T(8,128)}), f32[32,5248]{1,0:T(8,128)}) %all-reduce.14.cloned.1.call-update) | async-done | bytes 671760 | tf_op jit(solution)/shard_map/psum | solution.py:52
  545.8 1.0 slice_reduce_fusion
  546.7 1.4 multiply_reduce_fusion.5
  548.3 37.1 %psum.47 = f32[32,1]{1,0:T(8,128)S(1)} all-reduce(f32[32,1]{1,0:T(8,128)S(1)} %copy.27), channel_id=1, replica_groups=mesh['samp'=4,'snp'=8] {'snp'}, use_global_device_ids=true, to_apply=%region_18.0 | all-reduce | flops 32 | bytes 256 | tf_op jit(solution)/shard_map/psum | solution.py:71
  585.3 1.0 fusion.65
  586.3 2.3 add_multiply_fusion
  588.6 1.8 fusion.51
  (44 shorter events, 7.8 us)
Async XLA Ops:
  7.2 47.5 %all-gather.2.cloned.1.call-start = ((), (), s32[]{:S(2)}) async-start(), calls=%async_computation | async-start | bytes 1474560 | tf_op jit(solution)/shard_map/all_gather | solution.py:43
  7.9 118.5 %all-reduce.6.cloned.1.call-start = ((), (), s32[]{:S(2)}) async-start(), calls=%async_computation.1 | async-start | bytes 1343488 | tf_op jit(solution)/shard_map/psum | solution.py:52
  92.4 1.2 copy-start.4
  92.4 34.9 %copy-start.3 = (f32[5120]{0:T(1024)S(1)}, f32[5120]{0:T(1024)}, u32[]{:S(2)}) copy-start(f32[5120]{0:T(1024)} %param.5) | copy-start | bytes 61444
  93.5 162.8 %all-reduce.8.cloned.1.call-start = ((), (), s32[]{:S(2)}) async-start(), calls=%async_computation.2 | async-start | bytes 2654208 | tf_op jit(solution)/shard_map/psum | solution.py:68
  172.1 85.1 %copy-start = (f32[32,10240]{1,0:T(8,128)S(1)}, f32[32,10240]{1,0:T(8,128)}, u32[]{:S(2)}) copy-start(f32[32,10240]{1,0:T(8,128)} %all-gather.2.cloned.1.call-done) | copy-start | bytes 3932164
  172.1 161.0 %all-reduce.10.cloned.1.call-start = ((), (), s32[]{:S(2)}) async-start(), calls=%async_computation.3 | async-start | bytes 1343488 | tf_op jit(solution)/shard_map/psum | solution.py:52
  299.9 167.4 %all-reduce.12.cloned.1.call-start = ((), (), s32[]{:S(2)}) async-start(), calls=%async_computation.4 | async-start | bytes 2654208 | tf_op jit(solution)/shard_map/psum | solution.py:68
  383.2 162.6 %all-reduce.14.cloned.1.call-start = ((), (), s32[]{:S(2)}) async-start(), calls=%async_computation.5 | async-start | bytes 1343488 | tf_op jit(solution)/shard_map/psum | solution.py:52
  471.6 1.5 copy-start.2
  512.5 72.8 %copy-start.1 = (f32[32,5248]{1,0:T(8,128)S(1)}, f32[32,5248]{1,0:T(8,128)}, u32[]{:S(2)}) copy-start(f32[32,5248]{1,0:T(8,128)} %all-reduce.6.cloned.1.call-done) | copy-start | bytes 2015236
Sparse Core Ops, SparseCore 0:
  10.2 44.5 all-gather.1
  93.6 32.7 all-reduce.5
  172.2 84.0 all-reduce.7
  300.0 33.0 all-reduce.9
  383.3 83.9 all-reduce.11
  512.7 33.0 all-reduce.13
where the time goes:
time: 599 us; the launch traced here: 597 us
  waiting for transfers between devices  315 us (53%)
  matrix products  190 us (32%)
  blocking collectives  37.1 us (6%)
  other arithmetic  30.7 us (5%)
  between operations  14.2 us (2%)
  local copies, waits for them, and re-layouts  10.3 us (2%)
    dot_general x5, matrix products, product(): lax.dot_general(pieces, genotype, (((1,), (dimension,)), ((), ())), prefe...  190 us
    psum x2, waiting for transfers between devices, local(): summed = lax.psum(with_scalars(image, [power]), 'snp')  168 us
    psum x3, waiting for transfers between devices, local(): total = lax.psum(with_scalars(raw, scalars), 'samp')  99.1 us
    all_gather x1, waiting for transfers between devices, local(): residual = lax.all_gather(pheno_probes, 'snp', axis=1, tiled=True)  46.8 us
    psum x1, blocking collectives, local(): power = lax.psum(power, 'snp')  37.1 us
  transfers between devices with their start and end apart: 6, of which 6 were waited for; matrix products, arithmetic and copies ran while one was open for 0% of the time, Pallas kernels for 0%

commit v1 on v0

--- a/solution.py
+++ b/solution.py
@@ -40,7 +40,14 @@
     first = lax.axis_index("snp") * shard
     inverse = 1.0 / spread[None, :]
     middle = centre[None, :]
-    residual = lax.all_gather(pheno_probes, "snp", axis=1, tiled=True)
+    size = lax.axis_size("snp")
+    forward = [(i, (i + 1) % size) for i in range(size)]
+    parts = [pheno_probes]
+    for hop in range(1, size):
+        parts = [lax.ppermute(parts[0], "snp", forward), *parts]
+    full = jnp.concatenate(parts, axis=1)
+    shift = (lax.axis_index("snp") + 1) * parts[-1].shape[1]
+    residual = jnp.roll(full, shift, axis=1)
     direction = load = norm = square = None
     solution = stats = None
     for counter in range(ROUNDS):

time: 599 us -> 606 us (1.012)
  waiting for transfers between devices: 315 us -> 323 us
    ppermute x0 -> x7, waiting for transfers between devices: none -> 56.5 us  [local(): parts = [lax.ppermute(parts[0], 'snp', forward), *parts]]
    all_gather x1 -> x0, waiting for transfers between devices: 46.8 us -> none  [local(): residual = lax.all_gather(pheno_probes, 'snp', axis=1, tiled=True)]
  transfers between devices with their start and end apart: 6 -> 12, of which waited for: 6 -> 12; matrix products, arithmetic and copies ran while one was open for 0% -> 0% of each run, Pallas kernels for 0% -> 0%
where the time goes in v1:
time: 606 us; the launch traced here: 605 us
  waiting for transfers between devices  323 us (53%)
  matrix products  191 us (32%)
  blocking collectives  37.1 us (6%)
  other arithmetic  26.6 us (4%)
  between operations  14.1 us (2%)
  local copies, waits for them, and re-layouts  10.5 us (2%)
    dot_general x5, matrix products, product(): lax.dot_general(pieces, genotype, (((1,), (dimension,)), ((), ())), prefe...  191 us
    psum x2, waiting for transfers between devices, local(): summed = lax.psum(with_scalars(image, [power]), 'snp')  168 us
    psum x3, waiting for transfers between devices, local(): total = lax.psum(with_scalars(raw, scalars), 'samp')  98.4 us
    ppermute x7, waiting for transfers between devices, local(): parts = [lax.ppermute(parts[0], 'snp', forward), *parts]  56.5 us
    psum x1, blocking collectives, local(): power = lax.psum(power, 'snp')  37.1 us
  transfers between devices with their start and end apart: 12, of which 12 were waited for; matrix products, arithmetic and copies ran while one was open for 0% of the time, Pallas kernels for 0%

profile of v1, /device:TPU:0, one launch (start us, length us, event | category | flops | bytes accessed | tf_op | source)
XLA Modules:
  0.0 605.4 jit_solution(8926649795794939985)
XLA Ops:
  7.2 3.0 collective-permute-start
  10.3 7.4 %collective-permute-done = f32[32,1280]{1,0:T(8,128)S(1)} collective-permute-done((f32[32,1280]{1,0:T(8,128)}, f32[32,1280]{1,0:T(8,128)S(1)}, u32[]{:S(2)}, u32[]{:S(2)}) %collective-permute-start) | collective-permute-done | bytes 163872 | tf_op jit(solution)/shard_map/ppermute | solution.py:47
  17.7 8.1 %collective-permute-done.1 = f32[32,1280]{1,0:T(8,128)S(1)} collective-permute-done((f32[32,1280]{1,0:T(8,128)S(1)}, f32[32,1280]{1,0:T(8,128)S(1)}, u32[]{:S(2)}, u32[]{:S(2)}) %collective-permute-start.1) | collective-permute-done | bytes 163872 | tf_op jit(solution)/shard_map/ppermute | solution.py:47
  25.8 8.0 %collective-permute-done.2 = f32[32,1280]{1,0:T(8,128)S(1)} collective-permute-done((f32[32,1280]{1,0:T(8,128)S(1)}, f32[32,1280]{1,0:T(8,128)S(1)}, u32[]{:S(2)}, u32[]{:S(2)}) %collective-permute-start.2) | collective-permute-done | bytes 163872 | tf_op jit(solution)/shard_map/ppermute | solution.py:47
  33.8 8.0 %collective-permute-done.3 = f32[32,1280]{1,0:T(8,128)S(1)} collective-permute-done((f32[32,1280]{1,0:T(8,128)S(1)}, f32[32,1280]{1,0:T(8,128)S(1)}, u32[]{:S(2)}, u32[]{:S(2)}) %collective-permute-start.3) | collective-permute-done | bytes 163872 | tf_op jit(solution)/shard_map/ppermute | solution.py:47
  41.8 8.0 %collective-permute-done.4 = f32[32,1280]{1,0:T(8,128)S(1)} collective-permute-done((f32[32,1280]{1,0:T(8,128)S(1)}, f32[32,1280]{1,0:T(8,128)S(1)}, u32[]{:S(2)}, u32[]{:S(2)}) %collective-permute-start.4) | collective-permute-done | bytes 163872 | tf_op jit(solution)/shard_map/ppermute | solution.py:47
  49.8 8.9 %collective-permute-done.5 = f32[32,1280]{1,0:T(8,128)S(1)} collective-permute-done((f32[32,1280]{1,0:T(8,128)S(1)}, f32[32,1280]{1,0:T(8,128)S(1)}, u32[]{:S(2)}, u32[]{:S(2)}) %collective-permute-start.5) | collective-permute-done | bytes 163872 | tf_op jit(solution)/shard_map/ppermute | solution.py:47
  58.7 8.0 %collective-permute-done.6 = f32[32,1280]{1,0:T(8,128)S(1)} collective-permute-done((f32[32,1280]{1,0:T(8,128)S(1)}, f32[32,1280]{1,0:T(8,128)S(1)}, u32[]{:S(2)}, u32[]{:S(2)}) %collective-permute-start.6) | collective-permute-done | bytes 163872 | tf_op jit(solution)/shard_map/ppermute | solution.py:47
  68.6 35.8 %fusion.17 = f32[64,5120]{1,0:T(8,128)S(1)} fusion(bf16[10240,5120]{1,0:T(8,128)(2,1)} %param.4, bf16[32,10240]{1,0:T(8,128)(2,1)S(1)} %get-tuple-element.22, bf16[32,10240]{1,0:T(8,128)(2,1)S(1)} %get-tuple-element.23), kind=kOutput, calls=%fused_computation.30 | convolution fusion | flops 6713507840 | bytes 107479040 | tf_op jit(solution)/shard_map/dot_general | solution.py:20
  105.7 32.0 %all-reduce.6.cloned.1.call-done = f32[32,5248]{1,0:T(8,128)} async-done(((f32[32,5248]{1,0:T(8,128)}), f32[32,5248]{1,0:T(8,128)}) %all-reduce.6.cloned.1.call-update) | async-done | bytes 671760 | tf_op jit(solution)/shard_map/psum | solution.py:59
  138.5 1.5 multiply_reduce_fusion.7
  140.1 39.7 %fusion.42 = f32[64,10240]{1,0:T(8,128)S(1)} fusion(bf16[10240,5120]{1,0:T(8,128)(2,1)} %param.4, bf16[32,5120]{1,0:T(8,128)(2,1)S(1)} %get-tuple-element.29, bf16[32,5120]{1,0:T(8,128)(2,1)S(1)} %get-tuple-element.28), kind=kOutput, calls=%fused_computation.73 | convolution fusion | flops 6712197120 | bytes 108134400 | tf_op jit(solution)/shard_map/dot_general | solution.py:20
  179.8 1.2 fusion.16
  181.1 2.3 concatenate.45
  183.6 83.9 %all-reduce.8.cloned.1.call-done = f32[32,10368]{1,0:T(8,128)} async-done(((f32[32,10368]{1,0:T(8,128)}), f32[32,10368]{1,0:T(8,128)}) %all-reduce.8.cloned.1.call-update) | async-done | bytes 1327120 | tf_op jit(solution)/shard_map/psum | solution.py:75
  268.4 2.6 multiply_reduce_fusion.2
  271.2 36.9 %fusion.21 = f32[64,5120]{1,0:T(8,128)} fusion(bf16[10240,5120]{1,0:T(8,128)(2,1)} %param.4, bf16[32,10240]{1,0:T(8,128)(2,1)S(1)} %get-tuple-element.27, bf16[32,10240]{1,0:T(8,128)(2,1)S(1)} %get-tuple-element.26), kind=kOutput, calls=%fused_computation.34 | convolution fusion | flops 6713507840 | bytes 107479040 | tf_op jit(solution)/shard_map/dot_general | solution.py:20
  308.1 1.4 slice_add_fusion.3
  310.7 33.2 %all-reduce.10.cloned.1.call-done = f32[32,5248]{1,0:T(8,128)} async-done(((f32[32,5248]{1,0:T(8,128)}), f32[32,5248]{1,0:T(8,128)}) %all-reduce.10.cloned.1.call-update) | async-done | bytes 671760 | tf_op jit(solution)/shard_map/psum | solution.py:59
  344.9 1.6 multiply_reduce_fusion.6
  346.7 42.4 %fusion.46 = f32[64,10240]{1,0:T(8,128)} fusion(bf16[10240,5120]{1,0:T(8,128)(2,1)} %param.4, bf16[32,5120]{1,0:T(8,128)(2,1)S(1)} %get-tuple-element.31, bf16[32,5120]{1,0:T(8,128)(2,1)S(1)} %get-tuple-element.30), kind=kOutput, calls=%fused_computation.77 | convolution fusion | flops 6712197120 | bytes 108134400 | tf_op jit(solution)/shard_map/dot_general | solution.py:20
  389.1 3.0 fusion.12
  392.0 2.2 concatenate.49
  394.6 83.9 %all-reduce.12.cloned.1.call-done = f32[32,10368]{1,0:T(8,128)} async-done(((f32[32,10368]{1,0:T(8,128)}), f32[32,10368]{1,0:T(8,128)}) %all-reduce.12.cloned.1.call-update) | async-done | bytes 1327120 | tf_op jit(solution)/shard_map/psum | solution.py:75
  479.5 3.7 multiply_reduce_fusion
  483.2 1.1 reduce-precision_convert_fusion
  484.6 36.0 %fusion.25 = f32[64,5120]{1,0:T(8,128)S(1)} fusion(bf16[10240,5120]{1,0:T(8,128)(2,1)} %param.4, bf16[32,10240]{1,0:T(8,128)(2,1)} %get-tuple-element.25, bf16[32,10240]{1,0:T(8,128)(2,1)S(1)} %get-tuple-element.24), kind=kOutput, calls=%fused_computation.38 | convolution fusion | flops 6713507840 | bytes 107479040 | tf_op jit(solution)/shard_map/dot_general | solution.py:20
  521.9 33.2 %all-reduce.14.cloned.1.call-done = f32[32,5248]{1,0:T(8,128)} async-done(((f32[32,5248]{1,0:T(8,128)}), f32[32,5248]{1,0:T(8,128)}) %all-reduce.14.cloned.1.call-update) | async-done | bytes 671760 | tf_op jit(solution)/shard_map/psum | solution.py:59
  556.2 1.4 multiply_reduce_fusion.5
  557.7 37.1 %psum.47 = f32[32,1]{1,0:T(8,128)S(1)} all-reduce(f32[32,1]{1,0:T(8,128)S(1)} %copy.27), channel_id=1, replica_groups=mesh['samp'=4,'snp'=8] {'snp'}, use_global_device_ids=true, to_apply=%region_18.19 | all-reduce | flops 32 | bytes 256 | tf_op jit(solution)/shard_map/psum | solution.py:78
  595.8 1.9 fusion.51
  597.7 1.2 add_multiply_fusion
  (75 shorter events, 12.6 us)
Async XLA Ops:
  7.2 59.7 %copy-start.4 = (f32[32,1280]{1,0:T(8,128)S(1)}, f32[32,1280]{1,0:T(8,128)}, u32[]{:S(2)}) copy-start(f32[32,1280]{1,0:T(8,128)} %param.7) | copy-start | bytes 491524
  7.2 130.5 %all-reduce.6.cloned.1.call-start = ((), (), s32[]{:S(2)}) async-start(), calls=%async_computation | async-start | bytes 1343488 | tf_op jit(solution)/shard_map/psum | solution.py:59
  7.2 10.5 %collective-permute-start = (f32[32,1280]{1,0:T(8,128)}, f32[32,1280]{1,0:T(8,128)S(1)}, u32[]{:S(2)}, u32[]{:S(2)}) collective-permute-start(f32[32,1280]{1,0:T(8,128)} %param.7), channel_id=1, source_target_pairs={{0,1},{1,2},{2,3},{3,4},{4,5},{5,6},{6,7},{7,0},{8,9},{9,10},{10,1... | collective-permute-start | bytes 491528 | tf_op jit(solution)/shard_map/ppermute | solution.py:47
  17.7 8.1 %collective-permute-start.1 = (f32[32,1280]{1,0:T(8,128)S(1)}, f32[32,1280]{1,0:T(8,128)S(1)}, u32[]{:S(2)}, u32[]{:S(2)}) collective-permute-start(f32[32,1280]{1,0:T(8,128)S(1)} %collective-permute-done), channel_id=1, source_target_pairs={{0,1},{1,2},{2,3},{3,4},{4,5},{5,6},{6,7},{7,0},{8,9},{9,10},{10,1... | collective-permute-start | bytes 491528 | tf_op jit(solution)/shard_map/ppermute | solution.py:47
  25.8 8.0 %collective-permute-start.2 = (f32[32,1280]{1,0:T(8,128)S(1)}, f32[32,1280]{1,0:T(8,128)S(1)}, u32[]{:S(2)}, u32[]{:S(2)}) collective-permute-start(f32[32,1280]{1,0:T(8,128)S(1)} %collective-permute-done.1), channel_id=1, source_target_pairs={{0,1},{1,2},{2,3},{3,4},{4,5},{5,6},{6,7},{7,0},{8,9},{9,10},{10,1... | collective-permute-start | bytes 491528 | tf_op jit(solution)/shard_map/ppermute | solution.py:47
  33.8 8.0 %collective-permute-start.3 = (f32[32,1280]{1,0:T(8,128)S(1)}, f32[32,1280]{1,0:T(8,128)S(1)}, u32[]{:S(2)}, u32[]{:S(2)}) collective-permute-start(f32[32,1280]{1,0:T(8,128)S(1)} %collective-permute-done.2), channel_id=1, source_target_pairs={{0,1},{1,2},{2,3},{3,4},{4,5},{5,6},{6,7},{7,0},{8,9},{9,10},{10,1... | collective-permute-start | bytes 491528 | tf_op jit(solution)/shard_map/ppermute | solution.py:47
  41.8 8.0 %collective-permute-start.4 = (f32[32,1280]{1,0:T(8,128)S(1)}, f32[32,1280]{1,0:T(8,128)S(1)}, u32[]{:S(2)}, u32[]{:S(2)}) collective-permute-start(f32[32,1280]{1,0:T(8,128)S(1)} %collective-permute-done.3), channel_id=1, source_target_pairs={{0,1},{1,2},{2,3},{3,4},{4,5},{5,6},{6,7},{7,0},{8,9},{9,10},{10,1... | collective-permute-start | bytes 491528 | tf_op jit(solution)/shard_map/ppermute | solution.py:47
  49.8 8.9 %collective-permute-start.5 = (f32[32,1280]{1,0:T(8,128)S(1)}, f32[32,1280]{1,0:T(8,128)S(1)}, u32[]{:S(2)}, u32[]{:S(2)}) collective-permute-start(f32[32,1280]{1,0:T(8,128)S(1)} %collective-permute-done.4), channel_id=1, source_target_pairs={{0,1},{1,2},{2,3},{3,4},{4,5},{5,6},{6,7},{7,0},{8,9},{9,10},{10,1... | collective-permute-start | bytes 491528 | tf_op jit(solution)/shard_map/ppermute | solution.py:47
  58.7 8.0 %collective-permute-start.6 = (f32[32,1280]{1,0:T(8,128)S(1)}, f32[32,1280]{1,0:T(8,128)S(1)}, u32[]{:S(2)}, u32[]{:S(2)}) collective-permute-start(f32[32,1280]{1,0:T(8,128)S(1)} %collective-permute-done.5), channel_id=1, source_target_pairs={{0,1},{1,2},{2,3},{3,4},{4,5},{5,6},{6,7},{7,0},{8,9},{9,10},{10,1... | collective-permute-start | bytes 491528 | tf_op jit(solution)/shard_map/ppermute | solution.py:47
  67.1 1.5 copy-start
  104.5 1.2 copy-start.6
  104.5 34.0 %copy-start.5 = (f32[5120]{0:T(1024)S(1)}, f32[5120]{0:T(1024)}, u32[]{:S(2)}) copy-start(f32[5120]{0:T(1024)} %param.5) | copy-start | bytes 61444
  105.6 161.9 %all-reduce.8.cloned.1.call-start = ((), (), s32[]{:S(2)}) async-start(), calls=%async_computation.1 | async-start | bytes 2654208 | tf_op jit(solution)/shard_map/psum | solution.py:75
  183.4 84.2 %copy-start.1 = (f32[32,5248]{1,0:T(8,128)S(1)}, f32[32,5248]{1,0:T(8,128)}, u32[]{:S(2)}) copy-start(f32[32,5248]{1,0:T(8,128)} %all-reduce.6.cloned.1.call-done) | copy-start | bytes 2015236
  183.4 160.5 %all-reduce.10.cloned.1.call-start = ((), (), s32[]{:S(2)}) async-start(), calls=%async_computation.2 | async-start | bytes 1343488 | tf_op jit(solution)/shard_map/psum | solution.py:59
  310.7 167.8 %all-reduce.12.cloned.1.call-start = ((), (), s32[]{:S(2)}) async-start(), calls=%async_computation.3 | async-start | bytes 2654208 | tf_op jit(solution)/shard_map/psum | solution.py:75
  394.3 160.8 %all-reduce.14.cloned.1.call-start = ((), (), s32[]{:S(2)}) async-start(), calls=%async_computation.4 | async-start | bytes 1343488 | tf_op jit(solution)/shard_map/psum | solution.py:59
  483.2 1.4 copy-start.2
  555.1 39.6 %copy-start.3 = (f32[32,5248]{1,0:T(8,128)S(1)}, f32[32,5248]{1,0:T(8,128)}, u32[]{:S(2)}) copy-start(f32[32,5248]{1,0:T(8,128)} %all-reduce.14.cloned.1.call-done) | copy-start | bytes 2015236
Sparse Core Ops, SparseCore 0:
  105.7 31.8 all-reduce.5
  183.5 83.9 all-reduce.7
  310.8 33.0 all-reduce.9
  394.4 83.9 all-reduce.11
  522.0 33.0 all-reduce.13
